TPU v7x, 32 devices: a whole 2x2x4 slice. The times are simulated.
32 devices in a mesh: rows: 16 (over z, y, x), feat: 2 (over core).
Axes of the slice: x: 2, y: 2, z: 4, core: 2. Of those that a mesh axis runs over, the one named last changes fastest.
Arguments:
- bin_words: int32 [32768, 128], P('rows', 'feat'), may hold values from -2147483648 to 2147483646, as said below
- gradient: bfloat16 [32768], P('rows'), may hold values from -6 to 6
- hessian: bfloat16 [32768], P('rows'), may hold values from 0.099609375 to 1
- leaf_id: int32 [32768], P('rows'), may hold values from 0 to 63
- small_side: int32 [32], replicated, may hold values from 0 to 1
- parent_hist: float32 [512, 64, 256], P(('feat', 'rows')), may hold values from -12 to 12
Outputs:
- smaller_hist: float32 [512, 64, 256], P(('feat', 'rows'))
- larger_hist: float32 [512, 64, 256], P(('feat', 'rows'))
- feature_gain: float32 [512, 32], P(('feat', 'rows'))
- best_gain: float32 [32], replicated
Inputs may be any that keep to these rules, and one draw needn't show every extreme that they name: `bin_words`: byte k of word w (bits 8 k to 8 k + 7) holds the code of feature 4 w + k; a feature's bin is that byte modulo 256.
All inputs are finite; a program needn't handle non-finite values.
Results may differ from a plain program's by a relative error of at most 0.0003.
Values may be sent and summed in bfloat16 or wider, within the bound.
A program may use at most 64 MiB of HBM per device.

v0:
```python
import jax
import jax.numpy as jnp
from jax import lax
from jax.sharding import PartitionSpec as P

ridge_term = 1.0


def row_weights(gradient, hessian, leaf_id, small_side):
    pair_ids = jnp.arange(small_side.shape[0], dtype=jnp.int32)
    member = (
        (leaf_id[:, None] // 2 == pair_ids[None, :]) & (leaf_id[:, None] % 2 == small_side[None, :])
    ).astype(jnp.float32)
    return jnp.concatenate(
        [
            gradient.astype(jnp.float32)[:, None] * member,
            hessian.astype(jnp.float32)[:, None] * member,
        ],
        axis=1,
    )


def gains_from_left(left_sums, totals, pair_count):
    grad_left = left_sums[:, :pair_count]
    hess_left = left_sums[:, pair_count:]
    grad_total = totals[:pair_count][None, :, None]
    hess_total = totals[pair_count:][None, :, None]
    split_gain = 0.5 * (
        grad_left * grad_left / (hess_left + ridge_term)
        + (grad_total - grad_left)
        * (grad_total - grad_left)
        / (hess_total - hess_left + ridge_term)
        - grad_total * grad_total / (hess_total + ridge_term)
    )
    return jnp.max(split_gain, axis=2)


def columns_histogram(word_rows, weights_t, bin_count):
    shifts = 8 * jnp.arange(4, dtype=jnp.int32)
    shifted = jnp.right_shift(word_rows[:, None, :], shifts[None, :, None])
    bin_codes = jnp.bitwise_and(shifted, bin_count - 1).reshape(
        word_rows.shape[0] * 4, word_rows.shape[1]
    )
    one_hot = (bin_codes[:, :, None] == lax.iota(jnp.int32, bin_count)[None, None, :]).astype(
        jnp.bfloat16
    )
    return jnp.einsum("cr,frb->fcb", weights_t, one_hot, preferred_element_type=jnp.float32)


def on_device(bin_words, gradient, hessian, leaf_id, small_side, parent_hist):
    pair_count = small_side.shape[0]
    bin_count = parent_hist.shape[2]
    device_count = lax.axis_size("rows")
    local_features = bin_words.shape[1] * 4 // device_count
    weights_full = row_weights(gradient, hessian, leaf_id, small_side)
    moved_words = lax.all_to_all(bin_words.T, "rows", split_axis=0, concat_axis=1, tiled=True)
    moved_values = lax.all_gather(jnp.stack([gradient, hessian]), "rows", axis=1, tiled=True)
    moved_leaves = lax.all_gather(leaf_id, "rows", axis=0, tiled=True)
    block_count = min(16, device_count)
    block_rows = moved_words.shape[1] // block_count

    def add_block(index, running):
        first = index * block_rows
        word_rows = lax.dynamic_slice_in_dim(moved_words, first, block_rows, 1)
        value_rows = lax.dynamic_slice_in_dim(moved_values, first, block_rows, 1)
        leaf_rows = lax.dynamic_slice_in_dim(moved_leaves, first, block_rows, 0)
        block_weights = (
            row_weights(value_rows[0], value_rows[1], leaf_rows, small_side).astype(jnp.bfloat16).T
        )
        return running + columns_histogram(word_rows, block_weights, bin_count)

    initial = jnp.zeros((local_features, 2 * pair_count, bin_count), jnp.float32)
    local_hist = lax.fori_loop(0, block_count, add_block, initial)
    totals = lax.psum(jnp.sum(weights_full, axis=0), "rows")
    lower_ones = (
        lax.iota(jnp.int32, bin_count)[:, None] <= lax.iota(jnp.int32, bin_count - 1)[None, :]
    ).astype(jnp.float32)
    left_sums = jnp.einsum("fcb,bt->fct", local_hist, lower_ones, precision=lax.Precision.HIGHEST)
    feature_gain = gains_from_left(left_sums, totals, pair_count)
    best_gain = lax.pmax(jnp.max(feature_gain, axis=0), ("rows", "feat"))
    return (local_hist, parent_hist - local_hist, feature_gain, best_gain)


def solution(mesh):
    placed = (
        P("rows", "feat"),
        P("rows"),
        P("rows"),
        P("rows"),
        P(),
        P(("feat", "rows"), None, None),
    )
    return jax.shard_map(
        on_device,
        mesh=mesh,
        in_specs=placed,
        out_specs=(
            P(("feat", "rows"), None, None),
            P(("feat", "rows"), None, None),
            P(("feat", "rows"), None),
            P(),
        ),
        check_vma=False,
    )
```

profile of v0, /device:TPU:0, one launch (start us, length us, event | category | flops | bytes accessed | tf_op | source)
XLA Modules:
  0.0 279.6 jit_solution(9038843346561640959)
XLA Ops:
  0.7 2.0 all_to_all.14
  2.7 8.3 %all-to-all-start = ((s32[16,4,2048]{2,1,0:T(4,128)}), s32[16,4,2048]{2,1,0:T(4,128)S(1)}, u32[]{:S(2)}, u32[]{:S(2)}) async-start(s32[16,4,2048]{2,1,0:T(4,128)} %all_to_all.14), calls=%async_computation | async-start | bytes 1048576 | tf_op jit(solution)/shard_map/all_to_all | solution.py:56
  11.4 42.4 %psum.7 = f32[64]{0:T(128)S(1)} all-reduce(f32[64]{0:T(128)S(1)} %maximum_reduce_fusion), channel_id=1, replica_groups=mesh['rows'=16,'feat'=2] {'rows'}, use_global_device_ids=true, to_apply=%region_3.4 | all-reduce | flops 64 | bytes 512 | tf_op jit(solution)/shard_map/psum | solution.py:74
  53.8 38.0 %all_gather.6 = s32[32768]{0:T(1024)S(1)} all-gather(s32[2048]{0:T(1024)S(1)} %copy-done.2), channel_id=1, replica_groups=mesh['rows'=16,'feat'=2] {'rows'}, dimensions={0}, use_global_device_ids=true | all-gather | bytes 139264 | tf_op jit(solution)/shard_map/all_gather | solution.py:58
  91.8 36.4 %all_gather.7 = bf16[2,32768]{1,0:T(2,128)(2,1)S(1)} all-gather(bf16[2,2048]{1,0:T(2,128)(2,1)S(1)} %pad_maximum_fusion), channel_id=1, replica_groups=mesh['rows'=16,'feat'=2] {'rows'}, dimensions={1}, use_global_device_ids=true | all-gather | bytes 139264 | tf_op jit(solution)/shard_map/all_gather | solution.py:57
  128.2 110.8 %while.16 = (s32[]{:T(128)}, f32[16,64,256]{2,1,0:T(8,128)S(1)}, s32[4,32768]{1,0:T(4,128)S(1)}, s32[32768]{0:T(1024)S(1)}, s32[32]{0:T(128)S(1)}, /*index=5*/bf...) while((s32[]{:T(128)}, f32[16,64,256]{2,1,0:T(8,128)S(1)}, ...), condition=%wide.region_1.2_spmd.clone, body=%wide.region_0.1_spmd.clone.sunk | while | flops 1083627520 | bytes 3601005 | solution.py:73
  128.8 6.3 %fusion.21 = f32[16,64,256]{2,1,0:T(8,128)S(1)} fusion(s32[16,2048]{1,0:T(8,128)S(1)} %shift-right-arithmetic_and_fusion.2, f32[16,64,256]{2,1,0:T(8,128)S(1)} %get-tuple-element.271, pred[]{:T(512)S(6)} %compare.21, bf16[2048,32]{0,1:T(8,128)(2,1)S(1)} %get-tuple-element.257, bf16[2048,32]{0,1:T(8,128)(2,1)S(1)} %get-tuple-element.258), kind=kOutput, calls=%fused_computation.4.clone.1 | convolution fusion | flops 1083179008 | bytes 2490369 | tf_op jit(solution)/shard_map/while/body/eval_jaxpr/cr,frb->fcb/dot_general | solution.py:47
  135.7 6.3 %fusion.21 = f32[16,64,256]{2,1,0:T(8,128)S(1)} fusion(s32[16,2048]{1,0:T(8,128)S(1)} %shift-right-arithmetic_and_fusion.2, f32[16,64,256]{2,1,0:T(8,128)S(1)} %get-tuple-element.271, pred[]{:T(512)S(6)} %compare.21, bf16[2048,32]{0,1:T(8,128)(2,1)S(1)} %get-tuple-element.257, bf16[2048,32]{0,1:T(8,128)(2,1)S(1)} %get-tuple-element.258), kind=kOutput, calls=%fused_computation.4.clone.1 | convolution fusion | flops 1083179008 | bytes 2490369 | tf_op jit(solution)/shard_map/while/body/eval_jaxpr/cr,frb->fcb/dot_general | solution.py:47
  142.6 6.3 %fusion.21 = f32[16,64,256]{2,1,0:T(8,128)S(1)} fusion(s32[16,2048]{1,0:T(8,128)S(1)} %shift-right-arithmetic_and_fusion.2, f32[16,64,256]{2,1,0:T(8,128)S(1)} %get-tuple-element.271, pred[]{:T(512)S(6)} %compare.21, bf16[2048,32]{0,1:T(8,128)(2,1)S(1)} %get-tuple-element.257, bf16[2048,32]{0,1:T(8,128)(2,1)S(1)} %get-tuple-element.258), kind=kOutput, calls=%fused_computation.4.clone.1 | convolution fusion | flops 1083179008 | bytes 2490369 | tf_op jit(solution)/shard_map/while/body/eval_jaxpr/cr,frb->fcb/dot_general | solution.py:47
  149.6 6.3 %fusion.21 = f32[16,64,256]{2,1,0:T(8,128)S(1)} fusion(s32[16,2048]{1,0:T(8,128)S(1)} %shift-right-arithmetic_and_fusion.2, f32[16,64,256]{2,1,0:T(8,128)S(1)} %get-tuple-element.271, pred[]{:T(512)S(6)} %compare.21, bf16[2048,32]{0,1:T(8,128)(2,1)S(1)} %get-tuple-element.257, bf16[2048,32]{0,1:T(8,128)(2,1)S(1)} %get-tuple-element.258), kind=kOutput, calls=%fused_computation.4.clone.1 | convolution fusion | flops 1083179008 | bytes 2490369 | tf_op jit(solution)/shard_map/while/body/eval_jaxpr/cr,frb->fcb/dot_general | solution.py:47
  156.5 6.3 %fusion.21 = f32[16,64,256]{2,1,0:T(8,128)S(1)} fusion(s32[16,2048]{1,0:T(8,128)S(1)} %shift-right-arithmetic_and_fusion.2, f32[16,64,256]{2,1,0:T(8,128)S(1)} %get-tuple-element.271, pred[]{:T(512)S(6)} %compare.21, bf16[2048,32]{0,1:T(8,128)(2,1)S(1)} %get-tuple-element.257, bf16[2048,32]{0,1:T(8,128)(2,1)S(1)} %get-tuple-element.258), kind=kOutput, calls=%fused_computation.4.clone.1 | convolution fusion | flops 1083179008 | bytes 2490369 | tf_op jit(solution)/shard_map/while/body/eval_jaxpr/cr,frb->fcb/dot_general | solution.py:47
  163.4 6.3 %fusion.21 = f32[16,64,256]{2,1,0:T(8,128)S(1)} fusion(s32[16,2048]{1,0:T(8,128)S(1)} %shift-right-arithmetic_and_fusion.2, f32[16,64,256]{2,1,0:T(8,128)S(1)} %get-tuple-element.271, pred[]{:T(512)S(6)} %compare.21, bf16[2048,32]{0,1:T(8,128)(2,1)S(1)} %get-tuple-element.257, bf16[2048,32]{0,1:T(8,128)(2,1)S(1)} %get-tuple-element.258), kind=kOutput, calls=%fused_computation.4.clone.1 | convolution fusion | flops 1083179008 | bytes 2490369 | tf_op jit(solution)/shard_map/while/body/eval_jaxpr/cr,frb->fcb/dot_general | solution.py:47
  170.3 6.3 %fusion.21 = f32[16,64,256]{2,1,0:T(8,128)S(1)} fusion(s32[16,2048]{1,0:T(8,128)S(1)} %shift-right-arithmetic_and_fusion.2, f32[16,64,256]{2,1,0:T(8,128)S(1)} %get-tuple-element.271, pred[]{:T(512)S(6)} %compare.21, bf16[2048,32]{0,1:T(8,128)(2,1)S(1)} %get-tuple-element.257, bf16[2048,32]{0,1:T(8,128)(2,1)S(1)} %get-tuple-element.258), kind=kOutput, calls=%fused_computation.4.clone.1 | convolution fusion | flops 1083179008 | bytes 2490369 | tf_op jit(solution)/shard_map/while/body/eval_jaxpr/cr,frb->fcb/dot_general | solution.py:47
  177.3 6.3 %fusion.21 = f32[16,64,256]{2,1,0:T(8,128)S(1)} fusion(s32[16,2048]{1,0:T(8,128)S(1)} %shift-right-arithmetic_and_fusion.2, f32[16,64,256]{2,1,0:T(8,128)S(1)} %get-tuple-element.271, pred[]{:T(512)S(6)} %compare.21, bf16[2048,32]{0,1:T(8,128)(2,1)S(1)} %get-tuple-element.257, bf16[2048,32]{0,1:T(8,128)(2,1)S(1)} %get-tuple-element.258), kind=kOutput, calls=%fused_computation.4.clone.1 | convolution fusion | flops 1083179008 | bytes 2490369 | tf_op jit(solution)/shard_map/while/body/eval_jaxpr/cr,frb->fcb/dot_general | solution.py:47
  184.2 6.3 %fusion.21 = f32[16,64,256]{2,1,0:T(8,128)S(1)} fusion(s32[16,2048]{1,0:T(8,128)S(1)} %shift-right-arithmetic_and_fusion.2, f32[16,64,256]{2,1,0:T(8,128)S(1)} %get-tuple-element.271, pred[]{:T(512)S(6)} %compare.21, bf16[2048,32]{0,1:T(8,128)(2,1)S(1)} %get-tuple-element.257, bf16[2048,32]{0,1:T(8,128)(2,1)S(1)} %get-tuple-element.258), kind=kOutput, calls=%fused_computation.4.clone.1 | convolution fusion | flops 1083179008 | bytes 2490369 | tf_op jit(solution)/shard_map/while/body/eval_jaxpr/cr,frb->fcb/dot_general | solution.py:47
  191.1 6.3 %fusion.21 = f32[16,64,256]{2,1,0:T(8,128)S(1)} fusion(s32[16,2048]{1,0:T(8,128)S(1)} %shift-right-arithmetic_and_fusion.2, f32[16,64,256]{2,1,0:T(8,128)S(1)} %get-tuple-element.271, pred[]{:T(512)S(6)} %compare.21, bf16[2048,32]{0,1:T(8,128)(2,1)S(1)} %get-tuple-element.257, bf16[2048,32]{0,1:T(8,128)(2,1)S(1)} %get-tuple-element.258), kind=kOutput, calls=%fused_computation.4.clone.1 | convolution fusion | flops 1083179008 | bytes 2490369 | tf_op jit(solution)/shard_map/while/body/eval_jaxpr/cr,frb->fcb/dot_general | solution.py:47
  198.1 6.3 %fusion.21 = f32[16,64,256]{2,1,0:T(8,128)S(1)} fusion(s32[16,2048]{1,0:T(8,128)S(1)} %shift-right-arithmetic_and_fusion.2, f32[16,64,256]{2,1,0:T(8,128)S(1)} %get-tuple-element.271, pred[]{:T(512)S(6)} %compare.21, bf16[2048,32]{0,1:T(8,128)(2,1)S(1)} %get-tuple-element.257, bf16[2048,32]{0,1:T(8,128)(2,1)S(1)} %get-tuple-element.258), kind=kOutput, calls=%fused_computation.4.clone.1 | convolution fusion | flops 1083179008 | bytes 2490369 | tf_op jit(solution)/shard_map/while/body/eval_jaxpr/cr,frb->fcb/dot_general | solution.py:47
  205.0 6.3 %fusion.21 = f32[16,64,256]{2,1,0:T(8,128)S(1)} fusion(s32[16,2048]{1,0:T(8,128)S(1)} %shift-right-arithmetic_and_fusion.2, f32[16,64,256]{2,1,0:T(8,128)S(1)} %get-tuple-element.271, pred[]{:T(512)S(6)} %compare.21, bf16[2048,32]{0,1:T(8,128)(2,1)S(1)} %get-tuple-element.257, bf16[2048,32]{0,1:T(8,128)(2,1)S(1)} %get-tuple-element.258), kind=kOutput, calls=%fused_computation.4.clone.1 | convolution fusion | flops 1083179008 | bytes 2490369 | tf_op jit(solution)/shard_map/while/body/eval_jaxpr/cr,frb->fcb/dot_general | solution.py:47
  211.9 6.3 %fusion.21 = f32[16,64,256]{2,1,0:T(8,128)S(1)} fusion(s32[16,2048]{1,0:T(8,128)S(1)} %shift-right-arithmetic_and_fusion.2, f32[16,64,256]{2,1,0:T(8,128)S(1)} %get-tuple-element.271, pred[]{:T(512)S(6)} %compare.21, bf16[2048,32]{0,1:T(8,128)(2,1)S(1)} %get-tuple-element.257, bf16[2048,32]{0,1:T(8,128)(2,1)S(1)} %get-tuple-element.258), kind=kOutput, calls=%fused_computation.4.clone.1 | convolution fusion | flops 1083179008 | bytes 2490369 | tf_op jit(solution)/shard_map/while/body/eval_jaxpr/cr,frb->fcb/dot_general | solution.py:47
  218.8 6.3 %fusion.21 = f32[16,64,256]{2,1,0:T(8,128)S(1)} fusion(s32[16,2048]{1,0:T(8,128)S(1)} %shift-right-arithmetic_and_fusion.2, f32[16,64,256]{2,1,0:T(8,128)S(1)} %get-tuple-element.271, pred[]{:T(512)S(6)} %compare.21, bf16[2048,32]{0,1:T(8,128)(2,1)S(1)} %get-tuple-element.257, bf16[2048,32]{0,1:T(8,128)(2,1)S(1)} %get-tuple-element.258), kind=kOutput, calls=%fused_computation.4.clone.1 | convolution fusion | flops 1083179008 | bytes 2490369 | tf_op jit(solution)/shard_map/while/body/eval_jaxpr/cr,frb->fcb/dot_general | solution.py:47
  225.8 6.3 %fusion.21 = f32[16,64,256]{2,1,0:T(8,128)S(1)} fusion(s32[16,2048]{1,0:T(8,128)S(1)} %shift-right-arithmetic_and_fusion.2, f32[16,64,256]{2,1,0:T(8,128)S(1)} %get-tuple-element.271, pred[]{:T(512)S(6)} %compare.21, bf16[2048,32]{0,1:T(8,128)(2,1)S(1)} %get-tuple-element.257, bf16[2048,32]{0,1:T(8,128)(2,1)S(1)} %get-tuple-element.258), kind=kOutput, calls=%fused_computation.4.clone.1 | convolution fusion | flops 1083179008 | bytes 2490369 | tf_op jit(solution)/shard_map/while/body/eval_jaxpr/cr,frb->fcb/dot_general | solution.py:47
  232.7 6.3 %fusion.21 = f32[16,64,256]{2,1,0:T(8,128)S(1)} fusion(s32[16,2048]{1,0:T(8,128)S(1)} %shift-right-arithmetic_and_fusion.2, f32[16,64,256]{2,1,0:T(8,128)S(1)} %get-tuple-element.271, pred[]{:T(512)S(6)} %compare.21, bf16[2048,32]{0,1:T(8,128)(2,1)S(1)} %get-tuple-element.257, bf16[2048,32]{0,1:T(8,128)(2,1)S(1)} %get-tuple-element.258), kind=kOutput, calls=%fused_computation.4.clone.1 | convolution fusion | flops 1083179008 | bytes 2490369 | tf_op jit(solution)/shard_map/while/body/eval_jaxpr/cr,frb->fcb/dot_general | solution.py:47
  240.7 1.1 sub.45
  242.8 36.8 %pmax.7 = f32[32]{0:T(128)} all-reduce(f32[32]{0:T(128)S(1)} %get-tuple-element.183), channel_id=1, replica_groups=mesh['rows'=16,'feat'=2] {'rows','feat'}, use_global_device_ids=true, to_apply=%region_6.7 | all-reduce | flops 32 | bytes 256 | tf_op jit(solution)/shard_map/pmax | solution.py:80
  (201 shorter events, 10.8 us)
Async XLA Ops:
  0.6 10.4 %copy-start.4 = (bf16[2048]{0:T(1024)(128)(2,1)S(1)}, bf16[2048]{0:T(1024)(128)(2,1)}, u32[]{:S(2)}) copy-start(bf16[2048]{0:T(1024)(128)(2,1)} %param.9) | copy-start | bytes 12292
  0.6 10.4 %copy-start.5 = (bf16[2048]{0:T(1024)(128)(2,1)S(1)}, bf16[2048]{0:T(1024)(128)(2,1)}, u32[]{:S(2)}) copy-start(bf16[2048]{0:T(1024)(128)(2,1)} %param.10) | copy-start | bytes 12292
  0.7 10.5 %copy-start.2 = (s32[2048]{0:T(1024)S(1)}, s32[2048]{0:T(1024)}, u32[]{:S(2)}) copy-start(s32[2048]{0:T(1024)} %param.11) | copy-start | bytes 24580
  0.7 10.5 %copy-start.3 = (s32[32]{0:T(128)S(1)}, s32[32]{0:T(128)}, u32[]{:S(2)}) copy-start(s32[32]{0:T(128)} %param.12) | copy-start | bytes 388
  2.7 125.6 %all-to-all-start = ((s32[16,4,2048]{2,1,0:T(4,128)}), s32[16,4,2048]{2,1,0:T(4,128)S(1)}, u32[]{:S(2)}, u32[]{:S(2)}) async-start(s32[16,4,2048]{2,1,0:T(4,128)} %all_to_all.14), calls=%async_computation | async-start | bytes 1048576 | tf_op jit(solution)/shard_map/all_to_all | solution.py:56
  239.0 1.0 copy-start
  239.1 1.6 copy-start.1
where the time goes:
time: 281 us; the launch traced here: 280 us
  blocking collectives  154 us (55%)
  matrix products  102 us (36%)
  starting transfers between devices  8.34 us (3%)
  other arithmetic  7.65 us (3%)
  local copies, waits for them, and re-layouts  5.65 us (2%)
    dot_general x16, matrix products, columns_histogram(): jnp.einsum('cr,frb->fcb', weights_t, one_hot, preferred_element_type=jnp....  101 us
    psum x1, blocking collectives, on_device(): totals = lax.psum(jnp.sum(weights_full, axis=0), 'rows')  42.4 us
    all_gather x1, blocking collectives, on_device(): moved_leaves = lax.all_gather(leaf_id, 'rows', axis=0, tiled=True)  38 us
    pmax x1, blocking collectives, on_device(): best_gain = lax.pmax(jnp.max(feature_gain, axis=0), ('rows', 'feat'))  36.8 us
    all_gather x1, blocking collectives, on_device(): lax.all_gather(jnp.stack([gradient, hessian]), 'rows', axis=1, tiled=True)  36.4 us
    all_to_all x1, starting transfers between devices, on_device(): lax.all_to_all(bin_words.T, 'rows', split_axis=0, concat_axis=1, tiled=True)  8.34 us
  transfers between devices with their start and end apart: 1, of which 0 were waited for; matrix products, arithmetic and copies ran while one was open for 0% of the time, Pallas kernels for 0%

commit v1 on v0

v1 whole, which is shorter than its diff:
```python
import functools

import jax
import jax.numpy as jnp
from jax import lax
from jax.experimental import pallas as pl
from jax.experimental.pallas import tpu as pltpu
from jax.sharding import PartitionSpec as P

ridge_term = 1.0
MESH = pl.DeviceIdType.MESH
VMEM = pltpu.MemorySpace.VMEM


def gains_from_left(left_sums, totals, pair_count):
    grad_left = left_sums[:, :pair_count]
    hess_left = left_sums[:, pair_count:]
    grad_total = totals[:, :pair_count]
    hess_total = totals[:, pair_count:]
    split_gain = 0.5 * (
        grad_left * grad_left / (hess_left + ridge_term)
        + (grad_total - grad_left)
        * (grad_total - grad_left)
        / (hess_total - hess_left + ridge_term)
        - grad_total * grad_total / (hess_total + ridge_term)
    )
    return jnp.max(split_gain, axis=2)


def exchange_kernel(n, words_ref, vals_ref, words_out, vals_out, send_sem, recv_sem, own_sem):
    me = lax.axis_index("rows")
    barrier = pltpu.get_barrier_semaphore()

    def greet(d, carry):
        peer = lax.rem(me + d, n)
        pl.semaphore_signal(barrier, inc=1, device_id={"rows": peer}, device_id_type=MESH)
        return carry

    lax.fori_loop(1, n, greet, 0)
    own_words = pltpu.make_async_copy(words_ref.at[me], words_out.at[me], own_sem.at[0])
    own_vals = pltpu.make_async_copy(vals_ref, vals_out.at[me], own_sem.at[1])
    own_words.start()
    own_vals.start()
    pl.semaphore_wait(barrier, n - 1)

    def copies(peer, slot):
        words = pltpu.make_async_remote_copy(
            src_ref=words_ref.at[peer],
            dst_ref=words_out.at[slot],
            send_sem=send_sem.at[0, peer],
            recv_sem=recv_sem.at[0, slot],
            device_id={"rows": peer},
            device_id_type=MESH,
        )
        vals = pltpu.make_async_remote_copy(
            src_ref=vals_ref,
            dst_ref=vals_out.at[slot],
            send_sem=send_sem.at[1, peer],
            recv_sem=recv_sem.at[1, slot],
            device_id={"rows": peer},
            device_id_type=MESH,
        )
        return words, vals

    def send(d, carry):
        words, vals = copies(lax.rem(me + d, n), me)
        words.start()
        vals.start()
        return carry

    lax.fori_loop(1, n, send, 0)
    own_words.wait()
    own_vals.wait()

    def finish(d, carry):
        peer = lax.rem(me + d, n)
        words, vals = copies(peer, peer)
        words.wait()
        vals.wait()
        return carry

    lax.fori_loop(1, n, finish, 0)


def exchange(words, vals, n):
    return pl.pallas_call(
        functools.partial(exchange_kernel, n),
        out_shape=(
            jax.ShapeDtypeStruct(words.shape, words.dtype),
            jax.ShapeDtypeStruct((n,) + vals.shape, vals.dtype),
        ),
        in_specs=[pl.BlockSpec(memory_space=VMEM)] * 2,
        out_specs=[pl.BlockSpec(memory_space=VMEM)] * 2,
        scratch_shapes=[
            pltpu.SemaphoreType.DMA((2, n)),
            pltpu.SemaphoreType.DMA((2, n)),
            pltpu.SemaphoreType.DMA((2,)),
        ],
        compiler_params=pltpu.CompilerParams(collective_id=0, has_side_effects=True),
        name="exchange",
    )(words, vals)


def add_block(words, vals, hist_ref, bins, weights, lanes_of, half, pairs):
    f32, bf16 = jnp.float32, jnp.bfloat16
    rows = words.shape[1]
    per_word = bins.shape[0] // words.shape[0]
    words_count = words.shape[0]
    for k in range(per_word):
        code = jnp.bitwise_and(jnp.right_shift(words, 8 * k), 2 * half - 1)
        bins[k * words_count : (k + 1) * words_count, :] = code.astype(f32)
    vals = vals.astype(f32)
    pair_row = jnp.broadcast_to(vals[2:3, :], (pairs, rows))
    member = pair_row == lax.broadcasted_iota(jnp.int32, (pairs, rows), 0).astype(f32)
    for c in range(2):
        column = jnp.broadcast_to(vals[c : c + 1, :], (pairs, rows))
        weights[c * pairs : (c + 1) * pairs, :] = jnp.where(member, column, 0.0).astype(bf16)

    def one_feature(w, k):
        row = jnp.broadcast_to(bins[pl.ds(k * words_count + w, 1), :], (16, rows))
        upper = row >= half
        low = jnp.where(upper, row - half, row).astype(bf16)
        top = jnp.where(upper, 1.0, 0.0).astype(bf16)
        low = jnp.concatenate([low] * (half // 16), axis=0)
        top = jnp.concatenate([top] * (2 * pairs // 16), axis=0)
        one_hot = jnp.where(low == lanes_of[...], jnp.bfloat16(1), jnp.bfloat16(0))
        held = weights[...]
        is_top = top > jnp.bfloat16(0.5)
        zero = jnp.zeros_like(held)
        split = jnp.concatenate(
            [jnp.where(is_top, zero, held), jnp.where(is_top, held, zero)], axis=0
        )
        part = lax.dot_general(
            split, one_hot, (((1,), (1,)), ((), ())), preferred_element_type=f32
        )
        f = w * per_word + k
        hist_ref[f, :, :half] += part[: 2 * pairs]
        hist_ref[f, :, half:] += part[2 * pairs :]

    def one_word(w, carry):
        for k in range(per_word):
            one_feature(w, k)
        return carry

    lax.fori_loop(0, words_count, one_word, 0)


def fill_lanes(lanes_of):
    lanes_of[...] = (
        lax.broadcasted_iota(jnp.int32, lanes_of.shape, 0).astype(jnp.float32).astype(jnp.bfloat16)
    )


def histogram_kernel(n, half, pairs, words_ref, vals_ref, hist_ref, bins, weights, lanes_of):
    fill_lanes(lanes_of)
    hist_ref[...] = jnp.zeros_like(hist_ref)

    def block(s, carry):
        add_block(words_ref[s], vals_ref[s], hist_ref, bins, weights, lanes_of, half, pairs)
        return carry

    lax.fori_loop(0, n, block, 0)


def histogram(words, vals, pairs, bin_count):
    n, word_count, rows = words.shape
    features = word_count * 4
    half = bin_count // 2
    return pl.pallas_call(
        functools.partial(histogram_kernel, n, half, pairs),
        out_shape=jax.ShapeDtypeStruct((features, 2 * pairs, bin_count), jnp.float32),
        in_specs=[pl.BlockSpec(memory_space=VMEM)] * 2,
        out_specs=pl.BlockSpec(memory_space=VMEM),
        scratch_shapes=[
            pltpu.VMEM((features, rows), jnp.float32),
            pltpu.VMEM((2 * pairs, rows), jnp.bfloat16),
            pltpu.VMEM((half, rows), jnp.bfloat16),
        ],
        name="histogram",
    )(words, vals)


def maximum_kernel(n, m, best_ref, out_ref, slots, send_sem, recv_sem):
    me = lax.axis_index("rows") * m + lax.axis_index("feat")
    total = n * m
    barrier = pltpu.get_barrier_semaphore()

    def place(d):
        peer = lax.rem(me + d, total)
        return peer, {"rows": peer // m, "feat": lax.rem(peer, m)}

    def greet(d, carry):
        pl.semaphore_signal(barrier, inc=1, device_id=place(d)[1], device_id_type=MESH)
        return carry

    lax.fori_loop(1, total, greet, 0)
    pl.semaphore_wait(barrier, total - 1)

    def copy(d, slot):
        peer, where = place(d)
        return pltpu.make_async_remote_copy(
            src_ref=best_ref,
            dst_ref=slots.at[me if slot is None else slot],
            send_sem=send_sem.at[peer],
            recv_sem=recv_sem.at[me if slot is None else slot],
            device_id=where,
            device_id_type=MESH,
        )

    def send(d, carry):
        copy(d, None).start()
        return carry

    lax.fori_loop(1, total, send, 0)

    def finish(d, best):
        peer, _ = place(d)
        copy(d, peer).wait()
        return jnp.maximum(best, slots[peer])

    out_ref[...] = lax.fori_loop(1, total, finish, best_ref[...])


def all_maximum(best, n, m):
    return pl.pallas_call(
        functools.partial(maximum_kernel, n, m),
        out_shape=jax.ShapeDtypeStruct(best.shape, best.dtype),
        in_specs=[pl.BlockSpec(memory_space=VMEM)],
        out_specs=pl.BlockSpec(memory_space=VMEM),
        scratch_shapes=[
            pltpu.VMEM((n * m,) + best.shape, best.dtype),
            pltpu.SemaphoreType.DMA((n * m,)),
            pltpu.SemaphoreType.DMA((n * m,)),
        ],
        compiler_params=pltpu.CompilerParams(collective_id=1, has_side_effects=True),
        name="maximum",
    )(best)


def on_device(bin_words, gradient, hessian, leaf_id, small_side, parent_hist):
    pair_count = small_side.shape[0]
    bin_count = parent_hist.shape[2]
    n = lax.axis_size("rows")
    m = lax.axis_size("feat")
    rows, word_count = bin_words.shape
    words = bin_words.T.reshape(n, word_count // n, rows)
    pair_ids = jnp.arange(pair_count, dtype=jnp.int32)
    is_member = jnp.any(
        (pair_ids * 2 + small_side)[:, None] == leaf_id[None, :], axis=0
    )
    pair = jnp.where(is_member, leaf_id // 2, pair_count).astype(jnp.bfloat16)
    vals = jnp.stack([gradient, hessian, pair, jnp.zeros_like(gradient)])
    moved_words, moved_vals = exchange(words, vals, n)
    local_hist = histogram(moved_words, moved_vals, pair_count, bin_count)
    upper = (
        lax.iota(jnp.int32, bin_count)[:, None] <= lax.iota(jnp.int32, bin_count)[None, :]
    ).astype(jnp.float32)
    sums = jnp.einsum("fcb,bt->fct", local_hist, upper, precision=lax.Precision.HIGHEST)
    feature_gain = gains_from_left(sums[:, :, :-1], sums[:, :, -1:], pair_count)
    best = jnp.pad(jnp.max(feature_gain, axis=0), (0, 128 - pair_count))[None, :]
    best_gain = all_maximum(best, n, m)[0, :pair_count]
    return (local_hist, parent_hist - local_hist, feature_gain, best_gain)


def solution(mesh):
    placed = (
        P("rows", "feat"),
        P("rows"),
        P("rows"),
        P("rows"),
        P(),
        P(("feat", "rows"), None, None),
    )
    return jax.shard_map(
        on_device,
        mesh=mesh,
        in_specs=placed,
        out_specs=(
            P(("feat", "rows"), None, None),
            P(("feat", "rows"), None, None),
            P(("feat", "rows"), None),
            P(),
        ),
        check_vma=False,
    )
```

time: 281 us -> 98.9 us (0.35)
  blocking collectives: 154 us -> 0 us
  matrix products: 102 us -> 1.92 us
  Pallas kernels: 0 us -> 85.9 us
  starting transfers between devices: 8.34 us -> 0 us
  other arithmetic: 7.65 us -> 4.15 us
    dot_general x17 -> x1, matrix products: 102 us -> 1.92 us  [on_device(): jnp.einsum('fcb,bt->fct', local_hist, upper, precision=lax.Precision.HIGH...]
    pallas_call x0 -> x3, Pallas kernels: none -> 85.9 us  [the longest x1 50 us: histogram(): pl.pallas_call(functools.partial(histogram_kernel, n, half, pairs), out_s...]
    all_gather x2 -> x0, blocking collectives: 74.3 us -> none  [the longest x1 38 us: on_device(): moved_leaves = lax.all_gather(leaf_id, 'rows', axis=0, tiled=True)]
    psum x1 -> x0, blocking collectives: 42.4 us -> none  [on_device(): totals = lax.psum(jnp.sum(weights_full, axis=0), 'rows')]
    pmax x1 -> x0, blocking collectives: 36.8 us -> none  [on_device(): best_gain = lax.pmax(jnp.max(feature_gain, axis=0), ('rows', 'feat'))]
    all_to_all x1 -> x0, starting transfers between devices: 8.34 us -> none  [on_device(): lax.all_to_all(bin_words.T, 'rows', split_axis=0, concat_axis=1, tiled=True)]
  transfers between devices with their start and end apart: 1 -> 0, of which waited for: 0 -> 0; matrix products, arithmetic and copies ran while one was open for 0% -> 0% of each run, Pallas kernels for 0% -> 0%
where the time goes in v1:
time: 98.9 us; the launch traced here: 98.5 us
  Pallas kernels  85.9 us (87%)
  local copies, waits for them, and re-layouts  5.78 us (6%)
  other arithmetic  4.15 us (4%)
  matrix products  1.92 us (2%)
    pallas_call x1, Pallas kernels, histogram(): pl.pallas_call(functools.partial(histogram_kernel, n, half, pairs), out_s...  50 us
    pallas_call x1, Pallas kernels, exchange(): pl.pallas_call(functools.partial(exchange_kernel, n), out_shape=(jax.Shap...  22.1 us
    pallas_call x1, Pallas kernels, all_maximum(): pl.pallas_call(functools.partial(maximum_kernel, n, m), out_shape=jax.Sha...  13.8 us
    unnamed x12, local copies, waits for them, and re-layouts  2 us
    reshape x1, local copies, waits for them, and re-layouts, on_device(): words = bin_words.T.reshape(n, word_count // n, rows)  1.98 us

profile of v1, /device:TPU:0, one launch (start us, length us, event | category | flops | bytes accessed | tf_op | source)
XLA Modules:
  0.0 98.5 jit_solution(9786813357139344746)
XLA Ops:
  0.6 0.0 copy-start.5
  0.6 0.0 copy-start.2
  0.7 0.6 copy-done.5
  1.3 0.1 pad.8.clone
  1.4 0.8 compare_reduce_fusion
  2.2 0.0 copy-done.2
  2.2 0.0 copy-start.3
  2.2 0.7 copy-done.3
  2.9 0.0 copy-start.4
  2.9 0.7 copy-done.4
  3.6 0.7 maximum_maximum_fusion.vals_ref
  4.3 2.0 %reshape.13.words_ref = s32[16,4,2048]{2,1,0:T(4,128)} reshape(s32[64,2048]{1,0:T(8,128)} %bitcast.10) | data formatting | bytes 1048576 | tf_op jit(solution)/shard_map/reshape | solution.py:246
  6.3 22.1 %exchange.1 = (s32[16,4,2048]{2,1,0:T(4,128)}, bf16[16,4,2048]{2,1,0:T(4,128)(2,1)}) custom-call(s32[16,4,2048]{2,1,0:T(4,128)} %reshape.13.words_ref, bf16[4,2048]{1,0:T(4,128)(2,1)} %maximum_maximum_fusion.vals_ref), custom_call_target="tpu_custom_call" | custom-call | tf_op jit(solution)/shard_map/exchange/pallas_call | solution.py:86
  28.4 50.0 %histogram.1 = f32[16,64,256]{2,1,0:T(8,128)} custom-call(s32[16,4,2048]{2,1,0:T(4,128)} %get-tuple-element.6.words_ref, bf16[16,4,2048]{2,1,0:T(4,128)(2,1)} %get-tuple-element.7.vals_ref), custom_call_target="tpu_custom_call" | custom-call | tf_op jit(solution)/shard_map/histogram/pallas_call | solution.py:169
  78.3 1.9 %fusion.2 = f32[16,64,256]{2,1,0:T(8,128)S(1)} fusion(f32[16,64,256]{2,1,0:T(8,128)} %histogram.1), kind=kOutput, calls=%fused_computation.5 | convolution fusion | flops 805371904 | bytes 2097152 | tf_op jit(solution)/shard_map/fcb,bt->fct/dot_general | solution.py:258
  80.3 0.0 copy-start
  80.3 0.4 slice_reduce_fusion.1
  80.7 1.1 %fusion.8 = (f32[32]{0:T(128)S(1)}, f32[16,32]{1,0:T(8,128)}) fusion(f32[16,32]{1,0:T(8,128)S(1)} %get-tuple-element.9, f32[16,32]{1,0:T(8,128)S(1)} %get-tuple-element.10, f32[16,32]{1,0:T(8,128)S(1)} %get-tuple-element.8, f32[16,64,256]{2,1,0:T(8,128)S(1)} %fusion.2), kind=kLoop, calls=%fused_computation.22 | loop fusion | flops 1696736 | bytes 1052800 | tf_op jit(solution)/shard_map/reduce_max | solution.py:260
  81.8 0.5 pad_bitcast_fusion.best_ref
  82.3 13.8 %maximum.7 = f32[1,128]{1,0:T(1,128)} custom-call(f32[1,128]{1,0:T(1,128)} %pad_bitcast_fusion.best_ref), custom_call_target="tpu_custom_call" | custom-call | tf_op jit(solution)/shard_map/maximum/pallas_call | solution.py:225
  96.2 1.2 %slice_bitcast_fusion = f32[32]{0:T(128)} fusion(f32[1,128]{1,0:T(1,128)} %maximum.7), kind=kLoop, calls=%fused_computation.19 | loop fusion | bytes 256 | tf_op jit(solution)/shard_map/squeeze | solution.py:261
  97.3 0.0 copy-done.1
  97.4 0.0 copy-done
  97.4 1.1 %sub.44 = f32[16,64,256]{2,1,0:T(8,128)} subtract(f32[16,64,256]{2,1,0:T(8,128)S(1)} %copy-done.1, f32[16,64,256]{2,1,0:T(8,128)S(1)} %copy-done) | non-fusion elementwise | flops 262144 | bytes 3145728 | tf_op jit(solution)/shard_map/sub | solution.py:262
  (6 shorter events, 0.0 us)
Async XLA Ops:
  0.6 0.7 copy-start.5
  0.6 1.5 %copy-start.2 = (s32[2048]{0:T(1024)S(1)}, s32[2048]{0:T(1024)}, u32[]{:S(2)}) copy-start(s32[2048]{0:T(1024)} %param.9) | copy-start | bytes 24580
  2.2 0.7 copy-start.3
  2.9 0.7 copy-start.4
  78.3 19.0 %copy-start.1 = (f32[16,64,256]{2,1,0:T(8,128)S(1)}, f32[16,64,256]{2,1,0:T(8,128)}, u32[]{:S(2)}) copy-start(f32[16,64,256]{2,1,0:T(8,128)} %param.11) | copy-start | bytes 3145732
  80.3 17.1 %copy-start = (f32[16,64,256]{2,1,0:T(8,128)S(1)}, f32[16,64,256]{2,1,0:T(8,128)}, u32[]{:S(2)}) copy-start(f32[16,64,256]{2,1,0:T(8,128)} %histogram.1) | copy-start | bytes 3145732

commit v2 on v0

v2 whole, which is shorter than its diff:
```python
import functools

import jax
import jax.numpy as jnp
from jax import lax
from jax.experimental import pallas as pl
from jax.experimental.pallas import tpu as pltpu
from jax.sharding import PartitionSpec as P

ridge_term = 1.0
MESH = pl.DeviceIdType.MESH
VMEM = pltpu.MemorySpace.VMEM


def gains_from_left(left, pairs):
    grad_left, hess_left = left[:pairs], left[pairs:]
    last = left.shape[1] - 1
    grad_total, hess_total = grad_left[:, last:], hess_left[:, last:]
    gain = 0.5 * (
        grad_left * grad_left / (hess_left + ridge_term)
        + (grad_total - grad_left)
        * (grad_total - grad_left)
        / (hess_total - hess_left + ridge_term)
        - grad_total * grad_total / (hess_total + ridge_term)
    )
    lane = lax.broadcasted_iota(jnp.int32, gain.shape, 1)
    gain = jnp.where(lane < last, gain, -jnp.inf)
    best = gain[:, :128]
    for first in range(128, last + 1, 128):
        best = jnp.maximum(best, gain[:, first : first + 128])
    return best


def add_block(words, vals, hist_ref, bins, weights, lanes_of, half, pairs):
    f32, bf16 = jnp.float32, jnp.bfloat16
    rows = words.shape[1]
    per_word = bins.shape[0] // words.shape[0]
    words_count = words.shape[0]
    for k in range(per_word):
        code = jnp.bitwise_and(jnp.right_shift(words, 8 * k), 2 * half - 1)
        bins[k * words_count : (k + 1) * words_count, :] = code.astype(f32)
    vals = vals.astype(f32)
    pair_row = jnp.broadcast_to(vals[2:3, :], (pairs, rows))
    member = pair_row == lax.broadcasted_iota(jnp.int32, (pairs, rows), 0).astype(f32)
    for c in range(2):
        column = jnp.broadcast_to(vals[c : c + 1, :], (pairs, rows))
        weights[c * pairs : (c + 1) * pairs, :] = jnp.where(member, column, 0.0).astype(bf16)

    def one_feature(w, k):
        row = jnp.broadcast_to(bins[pl.ds(k * words_count + w, 1), :], (16, rows))
        upper = row >= half
        low = jnp.where(upper, row - half, row).astype(bf16)
        top = jnp.where(upper, 1.0, 0.0).astype(bf16)
        low = jnp.concatenate([low] * (half // 16), axis=0)
        top = jnp.concatenate([top] * (2 * pairs // 16), axis=0)
        one_hot = jnp.where(low == lanes_of[...], jnp.bfloat16(1), jnp.bfloat16(0))
        held = weights[...]
        is_top = top > jnp.bfloat16(0.5)
        zero = jnp.zeros_like(held)
        split = jnp.concatenate(
            [jnp.where(is_top, zero, held), jnp.where(is_top, held, zero)], axis=0
        )
        part = lax.dot_general(
            split, one_hot, (((1,), (1,)), ((), ())), preferred_element_type=f32
        )
        f = w * per_word + k
        hist_ref[f, :, :half] += part[: 2 * pairs]
        hist_ref[f, :, half:] += part[2 * pairs :]

    def one_word(w, carry):
        for k in range(per_word):
            one_feature(w, k)
        return carry

    lax.fori_loop(0, words_count, one_word, 0)


def fill_lanes(lanes_of):
    lanes_of[...] = (
        lax.broadcasted_iota(jnp.int32, lanes_of.shape, 0).astype(jnp.float32).astype(jnp.bfloat16)
    )


def histogram_kernel(
    n, m, half, pairs, words_ref, vals_ref, hist_ref, gain_ref, best_ref,
    words_in, vals_in, bins, weights, lanes_of, send_sem, recv_sem,
    best_own, best_in, best_send, best_recv,
):
    me = lax.axis_index("rows")
    place = me * m + lax.axis_index("feat")
    total = n * m
    barrier = pltpu.get_barrier_semaphore()

    def other(d):
        peer = lax.rem(place + d, total)
        return peer, {"rows": peer // m, "feat": lax.rem(peer, m)}

    def greet(d, carry):
        pl.semaphore_signal(barrier, inc=1, device_id=other(d)[1], device_id_type=MESH)
        return carry

    lax.fori_loop(1, total, greet, 0)

    def copies(peer, slot):
        words = pltpu.make_async_remote_copy(
            src_ref=words_ref.at[peer],
            dst_ref=words_in.at[slot],
            send_sem=send_sem.at[0, peer],
            recv_sem=recv_sem.at[0, slot],
            device_id={"rows": peer},
            device_id_type=MESH,
        )
        vals = pltpu.make_async_remote_copy(
            src_ref=vals_ref,
            dst_ref=vals_in.at[slot],
            send_sem=send_sem.at[1, peer],
            recv_sem=recv_sem.at[1, slot],
            device_id={"rows": peer},
            device_id_type=MESH,
        )
        return words, vals

    pl.semaphore_wait(barrier, total - 1)

    def send(d, carry):
        words, vals = copies(lax.rem(me + d, n), me)
        words.start()
        vals.start()
        return carry

    lax.fori_loop(1, n, send, 0)
    fill_lanes(lanes_of)
    hist_ref[...] = jnp.zeros_like(hist_ref)
    words_in[me] = words_ref[me]
    vals_in[me] = vals_ref[...]

    def block(d, carry):
        source = lax.rem(me - d + n, n)

        @pl.when(d > 0)
        def _():
            words, vals = copies(source, source)
            words.wait_recv()
            vals.wait_recv()

        add_block(words_in[source], vals_in[source], hist_ref, bins, weights, lanes_of, half, pairs)
        return carry

    lax.fori_loop(0, n, block, 0)

    bin_count = 2 * half
    upper = (
        lax.broadcasted_iota(jnp.int32, (bin_count, bin_count), 0)
        <= lax.broadcasted_iota(jnp.int32, (bin_count, bin_count), 1)
    ).astype(jnp.float32)
    per_word = hist_ref.shape[0] // words_ref.shape[1]

    def word_gain(w, carry):
        own = hist_ref[pl.ds(w * per_word, per_word)]
        left = jnp.dot(
            own.reshape(per_word * 2 * pairs, bin_count),
            upper,
            precision=lax.Precision.HIGHEST,
            preferred_element_type=jnp.float32,
        )
        each = [
            gains_from_left(left[k * 2 * pairs : (k + 1) * 2 * pairs], pairs)
            for k in range(per_word)
        ]
        best = jnp.max(jnp.concatenate(each, axis=0).T, axis=0, keepdims=True)
        gain_ref[pl.ds(w, 1), :] = best
        return carry

    lax.fori_loop(0, words_ref.shape[1], word_gain, 0)
    best_own[...] = jnp.max(gain_ref[...], axis=0, keepdims=True)

    def best_copy(d, slot):
        peer, where = other(d)
        return peer, pltpu.make_async_remote_copy(
            src_ref=best_own,
            dst_ref=best_in.at[place if slot is None else slot],
            send_sem=best_send.at[peer],
            recv_sem=best_recv.at[place if slot is None else slot],
            device_id=where,
            device_id_type=MESH,
        )

    def finish(d, carry):
        peer = lax.rem(me + d, n)
        words, vals = copies(peer, peer)
        words.wait_send()
        vals.wait_send()
        return carry

    lax.fori_loop(1, n, finish, 0)

    def best_start(d, carry):
        best_copy(d, None)[1].start()
        return carry

    lax.fori_loop(1, total, best_start, 0)

    def best_finish(d, best):
        peer = lax.rem(place - d + total, total)
        best_copy(total - d, peer)[1].wait()
        return jnp.maximum(best, best_in[peer])

    best_ref[...] = lax.fori_loop(1, total, best_finish, best_own[...])


def histogram(words, vals, pairs, bin_count, m):
    n, word_count, rows = words.shape
    features = word_count * 4
    half = bin_count // 2
    return pl.pallas_call(
        functools.partial(histogram_kernel, n, m, half, pairs),
        out_shape=(
            jax.ShapeDtypeStruct((features, 2 * pairs, bin_count), jnp.float32),
            jax.ShapeDtypeStruct((word_count, 4 * pairs), jnp.float32),
            jax.ShapeDtypeStruct((1, 4 * pairs), jnp.float32),
        ),
        in_specs=[pl.BlockSpec(memory_space=VMEM)] * 2,
        out_specs=[pl.BlockSpec(memory_space=VMEM)] * 3,
        scratch_shapes=[
            pltpu.VMEM(words.shape, words.dtype),
            pltpu.VMEM((n,) + vals.shape, vals.dtype),
            pltpu.VMEM((features, rows), jnp.float32),
            pltpu.VMEM((2 * pairs, rows), jnp.bfloat16),
            pltpu.VMEM((half, rows), jnp.bfloat16),
            pltpu.SemaphoreType.DMA((2, n)),
            pltpu.SemaphoreType.DMA((2, n)),
            pltpu.VMEM((1, 4 * pairs), jnp.float32),
            pltpu.VMEM((n * m, 1, 4 * pairs), jnp.float32),
            pltpu.SemaphoreType.DMA((n * m,)),
            pltpu.SemaphoreType.DMA((n * m,)),
        ],
        compiler_params=pltpu.CompilerParams(collective_id=0, has_side_effects=True),
        name="histogram",
    )(words, vals)


def on_device(bin_words, gradient, hessian, leaf_id, small_side, parent_hist):
    pair_count = small_side.shape[0]
    bin_count = parent_hist.shape[2]
    n = lax.axis_size("rows")
    m = lax.axis_size("feat")
    rows, word_count = bin_words.shape
    words = bin_words.T.reshape(n, word_count // n, rows)
    pair_ids = jnp.arange(pair_count, dtype=jnp.int32)
    is_member = jnp.any(
        (pair_ids * 2 + small_side)[:, None] == leaf_id[None, :], axis=0
    )
    pair = jnp.where(is_member, leaf_id // 2, pair_count).astype(jnp.bfloat16)
    vals = jnp.stack([gradient, hessian, pair, jnp.zeros_like(gradient)])
    local_hist, gains, best = histogram(words, vals, pair_count, bin_count, m)
    feature_gain = gains.reshape(-1, pair_count)
    best_gain = jnp.max(best.reshape(-1, pair_count), axis=0)
    return (local_hist, parent_hist - local_hist, feature_gain, best_gain)


def solution(mesh):
    placed = (
        P("rows", "feat"),
        P("rows"),
        P("rows"),
        P("rows"),
        P(),
        P(("feat", "rows"), None, None),
    )
    return jax.shard_map(
        on_device,
        mesh=mesh,
        in_specs=placed,
        out_specs=(
            P(("feat", "rows"), None, None),
            P(("feat", "rows"), None, None),
            P(("feat", "rows"), None),
            P(),
        ),
        check_vma=False,
    )
```

time: 281 us -> 78.3 us (0.28)
  blocking collectives: 154 us -> 0 us
  matrix products: 102 us -> 0 us
  Pallas kernels: 0 us -> 66.2 us
  starting transfers between devices: 8.34 us -> 0 us
    dot_general x17 -> x0, matrix products: 102 us -> none  [the longest x16 101 us: columns_histogram(): jnp.einsum('cr,frb->fcb', weights_t, one_hot, preferred_element_type=jnp....]
    all_gather x2 -> x0, blocking collectives: 74.3 us -> none  [the longest x1 38 us: on_device(): moved_leaves = lax.all_gather(leaf_id, 'rows', axis=0, tiled=True)]
    pallas_call x0 -> x1, Pallas kernels: none -> 66.2 us  [histogram(): pl.pallas_call(functools.partial(histogram_kernel, n, m, half, pairs), ou...]
    psum x1 -> x0, blocking collectives: 42.4 us -> none  [on_device(): totals = lax.psum(jnp.sum(weights_full, axis=0), 'rows')]
    pmax x1 -> x0, blocking collectives: 36.8 us -> none  [on_device(): best_gain = lax.pmax(jnp.max(feature_gain, axis=0), ('rows', 'feat'))]
    all_to_all x1 -> x0, starting transfers between devices: 8.34 us -> none  [on_device(): lax.all_to_all(bin_words.T, 'rows', split_axis=0, concat_axis=1, tiled=True)]
    reshape x0 -> x3, local copies, waits for them, and re-layouts: none -> 2.83 us  [the longest x1 2.07 us: on_device(): words = bin_words.T.reshape(n, word_count // n, rows)]
  transfers between devices with their start and end apart: 1 -> 0, of which waited for: 0 -> 0; matrix products, arithmetic and copies ran while one was open for 0% -> 0% of each run, Pallas kernels for 0% -> 0%
where the time goes in v2:
time: 78.3 us; the launch traced here: 78 us
  Pallas kernels  66.2 us (85%)
  local copies, waits for them, and re-layouts  5.89 us (8%)
  other arithmetic  5.19 us (7%)
    pallas_call x1, Pallas kernels, histogram(): pl.pallas_call(functools.partial(histogram_kernel, n, m, half, pairs), ou...  66.2 us
    unnamed x17, local copies, waits for them, and re-layouts  2.45 us
    sub x1, other arithmetic, on_device(): return (local_hist, parent_hist - local_hist, feature_gain, best_gain)  2.42 us
    reshape x1, local copies, waits for them, and re-layouts, on_device(): words = bin_words.T.reshape(n, word_count // n, rows)  2.07 us

profile of v2, /device:TPU:0, one launch (start us, length us, event | category | flops | bytes accessed | tf_op | source)
XLA Modules:
  0.0 78.0 jit_solution(9461451278665354895)
XLA Ops:
  0.6 0.0 copy-start.1
  0.6 0.0 copy-start.6
  0.7 2.1 %reshape.19.words_ref = s32[16,4,2048]{2,1,0:T(4,128)} reshape(s32[64,2048]{1,0:T(8,128)} %bitcast.2) | data formatting | bytes 1048576 | tf_op jit(solution)/shard_map/reshape | solution.py:248
  2.7 0.0 copy-done.6
  2.7 0.9 %compare_reduce_fusion = pred[2048]{0:T(1024)(128)(4,1)S(1)} fusion(s32[2048]{0:T(1024)} %param.9, s32[32]{0:T(128)S(1)} %multiply_add_fusion), kind=kLoop, calls=%fused_computation | loop fusion | flops 129024 | bytes 10368 | tf_op jit(solution)/shard_map/reduce_or | solution.py:250
  3.6 0.0 copy-done.2
  3.6 0.0 copy-start.3
  3.7 0.7 copy-done.3
  4.3 0.7 copy-done.4
  5.0 0.1 pad.3.clone
  5.1 0.7 maximum_maximum_fusion.vals_ref
  5.8 66.2 %histogram.1 = (f32[16,64,256]{2,1,0:T(8,128)}, f32[4,128]{1,0:T(4,128)}, f32[1,128]{1,0:T(1,128)}) custom-call(s32[16,4,2048]{2,1,0:T(4,128)} %reshape.19.words_ref, bf16[4,2048]{1,0:T(4,128)(2,1)} %maximum_maximum_fusion.vals_ref), custom_call_target="tpu_custom_call" | custom-call | tf_op jit(solution)/shard_map/histogram/pallas_call | solution.py:215
  72.0 0.0 copy-done.1
  72.0 0.0 copy-start.5
  72.0 0.0 copy-start
  72.0 2.4 %sub.10 = f32[16,64,256]{2,1,0:T(8,128)} subtract(f32[16,64,256]{2,1,0:T(8,128)S(1)} %copy-done.1, f32[16,64,256]{2,1,0:T(8,128)} %get-tuple-element.14) | non-fusion elementwise | flops 262144 | bytes 3145728 | tf_op jit(solution)/shard_map/sub | solution.py:258
  74.4 0.0 copy-done.5
  74.4 0.7 reshape.20
  75.1 0.5 broadcast.16
  75.6 0.1 copy-done.7
  75.7 0.7 reduce.3
  76.4 0.1 reshape.21
  76.5 0.5 reduce_max.9
  77.0 1.0 %copy.11 = f32[16,64,256]{2,1,0:T(8,128)} copy(f32[16,64,256]{2,1,0:T(8,128)S(1)} %copy-done) | data formatting | bytes 2097152
  (9 shorter events, 0.0 us)
Async XLA Ops:
  0.6 71.3 %copy-start.1 = (f32[16,64,256]{2,1,0:T(8,128)S(1)}, f32[16,64,256]{2,1,0:T(8,128)}, u32[]{:S(2)}) copy-start(f32[16,64,256]{2,1,0:T(8,128)} %param.11) | copy-start | bytes 3145732
  0.6 2.1 %copy-start.6 = (s32[32]{0:T(128)S(1)}, s32[32]{0:T(128)}, u32[]{:S(2)}) copy-start(s32[32]{0:T(128)} %param.10) | copy-start | bytes 388
  2.7 0.9 %copy-start.2 = (s32[2048]{0:T(1024)S(1)}, s32[2048]{0:T(1024)}, u32[]{:S(2)}) copy-start(s32[2048]{0:T(1024)} %param.9) | copy-start | bytes 24580
  3.6 0.7 copy-start.3
  4.3 0.7 copy-start.4
  72.0 2.4 %copy-start.5 = (f32[4,128]{1,0:T(4,128)S(1)}, f32[4,128]{1,0:T(4,128)}, u32[]{:S(2)}) copy-start(f32[4,128]{1,0:T(4,128)} %get-tuple-element.8) | copy-start | bytes 6148
  72.0 5.0 %copy-start = (f32[16,64,256]{2,1,0:T(8,128)S(1)}, f32[16,64,256]{2,1,0:T(8,128)}, u32[]{:S(2)}) copy-start(f32[16,64,256]{2,1,0:T(8,128)} %get-tuple-element.14) | copy-start | bytes 3145732
  75.1 0.6 copy-start.7
